TPU v7x, 32 devices: a whole 2x2x4 slice. The times are simulated.
32 devices in a mesh: row: 8 (over z, core), col: 4 (over y, x).
Axes of the slice: x: 2, y: 2, z: 4, core: 2. Of those that a mesh axis runs over, the one named last changes fastest.
Arguments:
- factor: bfloat16 [8192, 8192], P('row', 'col'), as said below
- sel_tiles: int32 [32], replicated, may hold values from 0 to 63, as said below
- coupling: bfloat16 [8192, 2048], P('col', 'row')
Outputs:
- root_inverse: float32 [8192, 8192], P('row', 'col')
- child_inverse: float32 [2048, 8192], P('col', 'row')
Inputs may be any that keep to these rules, and one draw needn't show every extreme that they name: sel_tiles holds 32 distinct tile indices in increasing order; rows of coupling outside the listed tiles are zero. factor is lower triangular with a diagonal between 1 and 1.5.
All inputs are finite; a program needn't handle non-finite values.
Results may differ from a plain program's by a relative error of at most 0.003.
Values may be sent and summed in bfloat16 or wider, within the bound.
A program may use at most 128 MiB of HBM per device.

v0:
```python
import jax
import jax.numpy as jnp
from jax import lax
from jax.sharding import PartitionSpec as P

TILE = 128


def from_root(value, axis, source):
    kept = jnp.where(lax.axis_index(axis) == source, value, 0).astype(value.dtype)
    return lax.psum(kept, axis)


def body(factor, sel_tiles, coupling):
    rows_here = factor.shape[0]
    row_index = lax.axis_index("row")
    whole = lax.all_gather(factor, "row", axis=0, tiled=True)
    ratio = lax.axis_size("row") // lax.axis_size("col")
    offset = row_index % ratio * rows_here
    piece = lax.dynamic_slice_in_dim(whole, offset, rows_here, 1)
    partner = from_root(piece, "col", row_index // ratio)
    gram = lax.dot_general(
        partner, whole, (((0,), (0,)), ((), ())), preferred_element_type=jnp.float32
    )
    coupling_full = lax.all_gather(coupling, "row", axis=1, tiled=True)
    rounded = gram.astype(jnp.bfloat16)
    global_rows = row_index * rows_here + jnp.arange(rows_here, dtype=jnp.int32)
    member = jnp.any((global_rows // TILE)[:, None] == sel_tiles[None, :], axis=1)
    summed = lax.psum_scatter(
        lax.dot_general(
            coupling_full, rounded, (((0,), (1,)), ((), ())), preferred_element_type=jnp.float32
        ),
        "col",
        scatter_dimension=0,
        tiled=True,
    )
    child = jnp.where(member[None, :], -summed, jnp.float32(0.0))
    return (gram, child)


def solution(mesh):
    placed = (P("row", "col"), P(), P("col", "row"))
    return jax.shard_map(
        body,
        mesh=mesh,
        in_specs=placed,
        out_specs=(P("row", "col"), P("col", "row")),
        check_vma=False,
    )
```

profile of v0, /device:TPU:0, one launch (start us, length us, event | category | flops | bytes accessed | tf_op | source)
XLA Modules:
  0.0 817.3 jit_solution(11417977400386051904)
XLA Ops:
  7.2 0.0 all-gather.3.cloned.1.call-start
  7.2 0.7 all-gather.3.cloned.1.call-update
  7.9 0.0 all-reduce.2.cloned.1.call-start
  8.0 293.0 %all-gather.3.cloned.1.call-done = bf16[8192,2048]{1,0:T(8,128)(2,1)} async-done(((bf16[1024,2048]{1,0:T(8,128)(2,1)}), bf16[8192,2048]{1,0:T(8,128)(2,1)}) %all-gather.3.cloned.1.call-update) | async-done | bytes 33554448 | tf_op jit(solution)/shard_map/all_gather | solution.py:17
  300.9 15.0 %dynamic-slice_select_fusion = bf16[8192,1024]{1,0:T(8,128)(2,1)} fusion(bf16[8192,2048]{1,0:T(8,128)(2,1)} %all-gather.3.cloned.1.call-done, s32[]{:T(128)S(6)} %select_n.38, pred[]{:T(512)S(6)} %eq.18), kind=kLoop, calls=%fused_computation | loop fusion | flops 8388608 | bytes 33554436 | tf_op jit(solution)/shard_map/jit(_where)/select_n | solution.py:10
  316.0 0.0 all-reduce.2.cloned.1.call-update
  316.0 0.0 all-gather.5.cloned.1.call-start
  316.0 0.7 all-gather.5.cloned.1.call-update
  316.7 0.0 reduce-scatter.2.cloned.1.call-start
  316.8 304.9 %all-reduce.2.cloned.1.call-done = bf16[8192,1024]{1,0:T(8,128)(2,1)} async-done(((bf16[8192,1024]{1,0:T(8,128)(2,1)}), bf16[8192,1024]{1,0:T(8,128)(2,1)}) %all-reduce.2.cloned.1.call-update) | async-done | bytes 16777232 | tf_op jit(solution)/shard_map/psum | solution.py:11
  621.7 43.9 %fusion.4 = f32[1024,2048]{1,0:T(8,128)} fusion(bf16[8192,1024]{1,0:T(8,128)(2,1)} %all-reduce.2.cloned.1.call-done, bf16[8192,2048]{1,0:T(8,128)(2,1)} %all-gather.3.cloned.1.call-done), kind=kOutput, calls=%fused_computation.14 | convolution fusion | flops 34359738368 | bytes 58720256 | tf_op jit(solution)/shard_map/dot_general | solution.py:22
  665.6 41.2 %all-gather.5.cloned.1.call-done = bf16[2048,2048]{1,0:T(8,128)(2,1)} async-done(((bf16[2048,256]{1,0:T(8,128)(2,1)}), bf16[2048,2048]{1,0:T(8,128)(2,1)}) %all-gather.5.cloned.1.call-update) | async-done | bytes 8388624 | tf_op jit(solution)/shard_map/all_gather | solution.py:25
  706.8 15.6 %convolution_bitcast_fusion = f32[2048,1024]{0,1:T(8,128)} fusion(bf16[2048,2048]{1,0:T(8,128)(2,1)} %all-gather.5.cloned.1.call-done, f32[1024,2048]{1,0:T(8,128)} %fusion.4), kind=kOutput, calls=%fused_computation.1 | convolution fusion | flops 8592031744 | bytes 25165824 | tf_op jit(solution)/shard_map/dot_general | solution.py:30
  722.4 0.0 copy-start
  722.4 0.0 reduce-scatter.2.cloned.1.call-update
  722.5 0.6 copy-done
  723.1 0.1 compare_reduce_fusion
  723.2 83.9 %reduce-scatter.2.cloned.1.call-done = f32[512,1024]{0,1:T(8,128)} async-done(((f32[2048,1024]{0,1:T(8,128)}), f32[512,1024]{0,1:T(8,128)}) %reduce-scatter.2.cloned.1.call-update) | async-done | bytes 2097168 | tf_op jit(solution)/shard_map/reduce_scatter | solution.py:29
  807.1 1.9 negate_select_fusion
  809.0 1.8 copy.6
  (1 shorter events, 0.0 us)
Async XLA Ops:
  7.2 293.8 %all-gather.3.cloned.1.call-start = ((), (), s32[]{:S(2)}) async-start(), calls=%async_computation.1 | async-start | bytes 37748736 | tf_op jit(solution)/shard_map/all_gather | solution.py:17
  7.9 613.8 %all-reduce.2.cloned.1.call-start = ((), (), s32[]{:S(2)}) async-start(), calls=%async_computation.2 | async-start | bytes 33554432 | tf_op jit(solution)/shard_map/psum | solution.py:11
  316.0 390.8 %all-gather.5.cloned.1.call-start = ((), (), s32[]{:S(2)}) async-start(), calls=%async_computation.3 | async-start | bytes 9437184 | tf_op jit(solution)/shard_map/all_gather | solution.py:25
  316.7 490.4 %reduce-scatter.2.cloned.1.call-start = ((), (), s32[]{:S(2)}) async-start(), calls=%async_computation.4 | async-start | bytes 10485760 | tf_op jit(solution)/shard_map/reduce_scatter | solution.py:29
  722.4 0.7 copy-start
Sparse Core Ops, SparseCore 0:
  9.6 291.3 all-gather.2
  316.1 305.5 all-reduce.1
  623.3 83.5 all-gather.4
  722.6 84.4 reduce-scatter.1
where the time goes:
time: 818 us; the launch traced here: 817 us
  waiting for transfers between devices  724 us (89%)
  matrix products  59.6 us (7%)
  other arithmetic  17 us (2%)
  between operations  13.8 us (2%)
    psum x1, waiting for transfers between devices, from_root(): return lax.psum(kept, axis)  305 us
    all_gather x1, waiting for transfers between devices, body(): whole = lax.all_gather(factor, 'row', axis=0, tiled=True)  293 us
    reduce_scatter x1, waiting for transfers between devices, body(): lax.psum_scatter(lax.dot_general(coupling_full, rounded, (((0,), (1,)), (...  83.9 us
    dot_general x1, matrix products, body(): lax.dot_general(partner, whole, (((0,), (0,)), ((), ())), preferred_eleme...  43.9 us
    all_gather x1, waiting for transfers between devices, body(): coupling_full = lax.all_gather(coupling, 'row', axis=1, tiled=True)  41.2 us
  transfers between devices with their start and end apart: 4, of which 4 were waited for; matrix products, arithmetic and copies ran while one was open for 5% of the time, Pallas kernels for 0%

commit v1 on v0

--- a/solution.py
+++ b/solution.py
@@ -22,7 +22,7 @@
     gram = lax.dot_general(
         partner, whole, (((0,), (0,)), ((), ())), preferred_element_type=jnp.float32
     )
-    coupling_full = lax.all_gather(coupling, "row", axis=1, tiled=True)
+    coupling_full = jnp.concatenate(lax.all_gather(coupling, "row"), axis=1)
     rounded = gram.astype(jnp.bfloat16)
     global_rows = row_index * rows_here + jnp.arange(rows_here, dtype=jnp.int32)
     member = jnp.any((global_rows // TILE)[:, None] == sel_tiles[None, :], axis=1)

time: 818 us -> 848 us (1.037)
  waiting for transfers between devices: 724 us -> 745 us
  local copies, waits for them, and re-layouts: 2.42 us -> 17.6 us
    all_gather x1, waiting for transfers between devices: 41.2 us -> 66.5 us  [body(): coupling_full = jnp.concatenate(lax.all_gather(coupling, 'row'), axis=1)]
    reshape x0 -> x1, local copies, waits for them, and re-layouts: none -> 11.8 us  [body(): coupling_full = jnp.concatenate(lax.all_gather(coupling, 'row'), axis=1)]
  transfers between devices with their start and end apart: 4 -> 4, of which waited for: 4 -> 4; matrix products, arithmetic and copies ran while one was open for 5% -> 3% of each run, Pallas kernels for 0% -> 0%
where the time goes in v1:
time: 848 us
  waiting for transfers between devices  745 us (88%)
  matrix products  54.4 us (6%)
  local copies, waits for them, and re-layouts  17.6 us (2%)
  other arithmetic  17.2 us (2%)
  between operations  13.8 us (2%)
    psum x1, waiting for transfers between devices, from_root(): return lax.psum(kept, axis)  298 us
    all_gather x1, waiting for transfers between devices, body(): whole = lax.all_gather(factor, 'row', axis=0, tiled=True)  292 us
    reduce_scatter x1, waiting for transfers between devices, body(): lax.psum_scatter(lax.dot_general(coupling_full, rounded, (((0,), (1,)), (...  86.8 us
    all_gather x1, waiting for transfers between devices, body(): coupling_full = jnp.concatenate(lax.all_gather(coupling, 'row'), axis=1)  66.5 us
    dot_general x1, matrix products, body(): lax.dot_general(partner, whole, (((0,), (0,)), ((), ())), preferred_eleme...  43.2 us
  transfers between devices with their start and end apart: 4, of which 4 were waited for; matrix products, arithmetic and copies ran while one was open for 3% of the time, Pallas kernels for 0%

profile of v1, /device:TPU:0, one launch (start us, length us, event | category | flops | bytes accessed | tf_op | source)
XLA Modules:
  0.0 847.9 jit_solution(12625466946509591858)
XLA Ops:
  7.2 0.0 all-gather.4.cloned.1.call-start
  7.2 0.7 all-gather.4.cloned.1.call-update
  7.9 0.0 all-gather.6.cloned.1.call-start
  7.9 0.7 all-gather.6.cloned.1.call-update
  8.6 0.0 all-reduce.2.cloned.1.call-start
  8.7 292.2 %all-gather.4.cloned.1.call-done = bf16[8192,2048]{1,0:T(8,128)(2,1)} async-done(((bf16[1024,2048]{1,0:T(8,128)(2,1)}), bf16[8192,2048]{1,0:T(8,128)(2,1)}) %all-gather.4.cloned.1.call-update) | async-done | bytes 33554448 | tf_op jit(solution)/shard_map/all_gather | solution.py:17
  300.9 15.3 %dynamic-slice_select_fusion = bf16[8192,1024]{1,0:T(8,128)(2,1)} fusion(bf16[8192,2048]{1,0:T(8,128)(2,1)} %all-gather.4.cloned.1.call-done, s32[]{:T(128)S(6)} %select_n.38, pred[]{:T(512)S(6)} %eq.18), kind=kLoop, calls=%fused_computation | loop fusion | flops 8388608 | bytes 33554436 | tf_op jit(solution)/shard_map/jit(_where)/select_n | solution.py:10
  316.2 0.0 all-reduce.2.cloned.1.call-update
  316.2 0.0 reduce-scatter.2.cloned.1.call-start
  316.3 66.5 %all-gather.6.cloned.1.call-done = bf16[16384,256]{1,0:T(8,128)(2,1)} async-done(((bf16[2048,256]{1,0:T(8,128)(2,1)}), bf16[16384,256]{1,0:T(8,128)(2,1)}) %all-gather.6.cloned.1.call-update) | async-done | bytes 8388624 | tf_op jit(solution)/shard_map/all_gather | solution.py:25
  382.8 11.8 %copy.9 = bf16[2048,8,256]{0,2,1:T(8,128)(2,1)} copy(bf16[2048,8,256]{2,0,1:T(8,128)(2,1)} %bitcast.9) | data formatting | bytes 16777216 | tf_op jit(solution)/shard_map/reshape | solution.py:25
  394.6 297.7 %all-reduce.2.cloned.1.call-done = bf16[8192,1024]{1,0:T(8,128)(2,1)} async-done(((bf16[8192,1024]{1,0:T(8,128)(2,1)}), bf16[8192,1024]{1,0:T(8,128)(2,1)}) %all-reduce.2.cloned.1.call-update) | async-done | bytes 16777232 | tf_op jit(solution)/shard_map/psum | solution.py:11
  692.3 0.0 copy-start
  692.3 43.2 %fusion.4 = f32[1024,2048]{1,0:T(8,128)S(1)} fusion(bf16[8192,1024]{1,0:T(8,128)(2,1)} %all-reduce.2.cloned.1.call-done, bf16[8192,2048]{1,0:T(8,128)(2,1)} %all-gather.4.cloned.1.call-done), kind=kOutput, calls=%fused_computation.14 | convolution fusion | flops 34359738368 | bytes 58720256 | tf_op jit(solution)/shard_map/dot_general | solution.py:22
  735.5 0.0 copy-start.2
  735.5 3.4 copy-done.2
  738.9 0.0 copy-done
  738.9 11.2 %convolution_bitcast_fusion = f32[2048,1024]{0,1:T(8,128)} fusion(bf16[2048,2048]{0,1:T(8,128)(2,1)S(1)} %bitcast.10, f32[1024,2048]{1,0:T(8,128)S(1)} %fusion.4), kind=kOutput, calls=%fused_computation.1 | convolution fusion | flops 8592031744 | bytes 25165824 | tf_op jit(solution)/shard_map/dot_general | solution.py:30
  750.1 0.0 copy-start.1
  750.1 0.0 reduce-scatter.2.cloned.1.call-update
  750.1 0.6 copy-done.1
  750.7 0.1 compare_reduce_fusion
  750.8 86.8 %reduce-scatter.2.cloned.1.call-done = f32[512,1024]{0,1:T(8,128)} async-done(((f32[2048,1024]{0,1:T(8,128)}), f32[512,1024]{0,1:T(8,128)}) %reduce-scatter.2.cloned.1.call-update) | async-done | bytes 2097168 | tf_op jit(solution)/shard_map/reduce_scatter | solution.py:29
  837.6 1.9 negate_select_fusion
  839.5 1.8 copy.10
  (1 shorter events, 0.0 us)
Async XLA Ops:
  7.2 293.8 %all-gather.4.cloned.1.call-start = ((), (), s32[]{:S(2)}) async-start(), calls=%async_computation.1 | async-start | bytes 37748736 | tf_op jit(solution)/shard_map/all_gather | solution.py:17
  7.9 374.9 %all-gather.6.cloned.1.call-start = ((), (), s32[]{:S(2)}) async-start(), calls=%async_computation.4 | async-start | bytes 9437184 | tf_op jit(solution)/shard_map/all_gather | solution.py:25
  8.6 683.6 %all-reduce.2.cloned.1.call-start = ((), (), s32[]{:S(2)}) async-start(), calls=%async_computation.2 | async-start | bytes 33554432 | tf_op jit(solution)/shard_map/psum | solution.py:11
  316.2 521.4 %reduce-scatter.2.cloned.1.call-start = ((), (), s32[]{:S(2)}) async-start(), calls=%async_computation.3 | async-start | bytes 10485760 | tf_op jit(solution)/shard_map/reduce_scatter | solution.py:29
  692.3 46.7 %copy-start = (bf16[2048,8,256]{0,2,1:T(8,128)(2,1)S(1)}, bf16[2048,8,256]{0,2,1:T(8,128)(2,1)}, u32[]{:S(2)}) copy-start(bf16[2048,8,256]{0,2,1:T(8,128)(2,1)} %copy.9) | copy-start | bytes 25165828
  735.5 3.4 copy-start.2
  750.1 0.7 copy-start.1
Sparse Core Ops, SparseCore 0:
  9.6 291.3 all-gather.3
  302.5 80.2 all-gather.5
  386.4 305.8 all-reduce.1
  750.2 87.3 reduce-scatter.1
